TPU v7x, 32 devices: a whole 2x2x4 slice. The times are simulated.
32 devices in a mesh: occ: 4 (over z), vsec: 4 (over y, core), aux: 2 (over x).
Axes of the slice: x: 2, y: 2, z: 4, core: 2. Of those that a mesh axis runs over, the one named last changes fastest.
Arguments:
- amplitudes: bfloat16 [16, 1024, 1024], P(('occ', 'vsec'), 'aux'), may hold values from -0.005859375 to 0.005859375
- left_factor: bfloat16 [4096, 8, 1024], P('aux', 'vsec'), may hold values from -0.75 to 0.75
- right_factor: bfloat16 [4096, 8, 1024], P('aux', None, 'occ'), may hold values from -0.75 to 0.75
- other_terms: float32 [16, 8, 8], P(('occ', 'aux'), 'vsec'), may hold values from -10.4 to 10.4
Outputs:
- residual: float32 [16, 8, 8], P(('occ', 'aux'), 'vsec')
- residual_norm: float32 [], replicated
All inputs are finite; a program needn't handle non-finite values.
Results may differ from a plain program's by a relative error of at most 0.002.
Values may be sent and summed in bfloat16 or wider, within the bound.
A program may use at most 192 MiB of HBM per device.

v0:
```python
import functools

import jax
import jax.numpy as jnp
from jax import lax
from jax.experimental import pallas as pl
from jax.experimental.pallas import tpu as pltpu
from jax.sharding import PartitionSpec as P

MESH = pl.DeviceIdType.MESH
ROWS = 256
COLS = 512
GROUP = 16
LANES = 128


def ladder_kernel(
    sizes, amps_ref, left_hbm, right_hbm, other_ref, res_ref, norm_ref,
    tbuf, left, right, left_t, high, low, acc, parts, norms,
    send_sem, recv_sem, load_sem, part_send, part_recv, norm_send, norm_recv,
):
    n_occ, n_sec, n_aux = sizes
    n_hi = n_sec // 2
    occ, sec, aux = lax.axis_index("occ"), lax.axis_index("vsec"), lax.axis_index("aux")
    hi, core = sec // 2, sec % 2
    pairs, virt, dsl = tbuf.shape
    half = amps_ref.shape[1]
    wide = right.shape[1]
    window = wide // dsl
    rows_ab = high.shape[0]

    load_l = pltpu.make_async_copy(left_hbm, left, load_sem.at[0])
    load_r = pltpu.make_async_copy(right_hbm, right, load_sem.at[1])
    load_l.start()
    load_r.start()

    def turn(value, step, count):
        found = turns.get((id(value), step))
        return lax.rem(value + step + count, count) if found is None else found

    turns = {}
    for value, count in ((occ, n_occ), (sec, n_sec), (aux, n_aux), (hi, n_hi)):
        for step in range(1 - count, count):
            turns[id(value), step] = lax.rem(value + (step + count), count)
    pair_at = {
        (k, j, far): turn(occ, -k, n_occ) * n_sec + turn(hi, -j, n_hi) * 2 + (1 - core if far else core)
        for k in range(n_occ) for j in range(n_hi) for far in (False, True)
    }
    half_at = [pl.multiple_of(turn(aux, -i, n_aux) * half, half) for i in range(n_aux)]
    partner = hi * 2 + 1 - core
    hi_to = [turn(hi, j, n_hi) * 2 + core for j in range(n_hi)]

    group = [(k, i) for k in range(n_occ) for i in range(n_aux) if (k, i) != (0, 0)]
    barrier = pltpu.get_barrier_semaphore()
    for k, i in group:
        pl.semaphore_signal(
            barrier, inc=1, device_id={"occ": turn(occ, k, n_occ), "aux": turn(aux, i, n_aux)},
            device_id_type=MESH,
        )
    for j in range(1, n_sec):
        pl.semaphore_signal(
            barrier, inc=1, device_id={"vsec": turn(sec, j, n_sec)}, device_id_type=MESH
        )
    pl.semaphore_wait(barrier, len(group) + n_sec - 1)

    ids = {}
    numbers = [occ * 0 + number for number in range(n_occ * n_sec * n_aux)]

    def sem_of(key):
        return numbers[ids.setdefault(key, len(ids))]

    def slot(k, j, i, far=False):
        return tbuf.at[pair_at[k, j, far], pl.ds(half_at[i], half), :]

    sent = []

    def send(src, dst, key, target):
        number = sem_of(key)
        copy = pltpu.make_async_remote_copy(
            src_ref=src, dst_ref=dst, send_sem=send_sem.at[number], recv_sem=recv_sem.at[number],
            device_id=target, device_id_type=MESH,
        )
        copy.start()
        sent.append(copy)

    def arrive(key, k, j, i, far=False):
        number = sem_of(key)
        ref = slot(k, j, i, far)
        pltpu.make_async_remote_copy(
            src_ref=ref, dst_ref=ref, send_sem=send_sem.at[number], recv_sem=recv_sem.at[number],
            device_id={"vsec": partner}, device_id_type=MESH,
        ).wait_recv()

    def to_core(src, k, j, i):
        send(src, slot(k, j, i), ("c", k, j, i), {"vsec": partner})

    def to_hi(src, dst, key, j):
        send(src, dst, key, {"vsec": hi_to[j]})

    def to_aux(src, dst, key, i):
        send(src, dst, key, {"aux": turn(aux, i, n_aux)})

    def spread(src, k):
        dst = slot(k, 0, 0)
        for j in range(1, n_hi):
            to_hi(src, dst, ("y", k, j), j)
        for i in range(1, n_aux):
            to_aux(src, dst, ("x", k, i), i)
        to_core(src, k, 0, 0)

    def own_slice(step):
        return amps_ref.at[0, :, pl.ds(pl.multiple_of(turn(occ, step, n_occ) * dsl, dsl), dsl)]

    order = sorted(range(1, n_occ), key=lambda k: (min(k, n_occ - k), k))
    for k in order:
        send(own_slice(k), slot(0, 0, 0), ("z", k), {"occ": turn(occ, k, n_occ)})
    spread(own_slice(0), 0)
    keep = pltpu.make_async_copy(own_slice(0), slot(0, 0, 0), load_sem.at[2])
    keep.start()

    def z_event(k):
        arrive(("z", k), k, 0, 0)
        spread(slot(k, 0, 0), k)

    def yx_event(k, turn_no):
        for j in range(1, n_hi):
            arrive(("y", k, j), k, j, 0)
            ref = slot(k, j, 0)
            if turn_no % 2 == 0:
                for i in range(1, n_aux):
                    to_aux(ref, ref, ("d", k, j, i), i)
            to_core(ref, k, j, 0)
        for i in range(1, n_aux):
            arrive(("x", k, i), k, 0, i)
            ref = slot(k, 0, i)
            if turn_no % 2 == 1:
                for j in range(1, n_hi):
                    to_hi(ref, ref, ("d", k, j, i), j)
            to_core(ref, k, 0, i)

    def d_event(k):
        for j in range(1, n_hi):
            for i in range(1, n_aux):
                arrive(("d", k, j, i), k, j, i)
                to_core(slot(k, j, i), k, j, i)

    every = [0] + order
    events = []
    for t, k in enumerate(every):
        if t + 1 < n_occ:
            events.append(functools.partial(z_event, every[t + 1]))
        events.append(functools.partial(yx_event, k, t))
        if t >= 1:
            events.append(functools.partial(d_event, every[t - 1]))
    events.append(functools.partial(d_event, every[-1]))

    load_l.wait()
    load_r.wait()
    n_m, n_n = left.shape[1] // ROWS, wide // COLS
    per_arow = virt // ROWS
    spots = n_m * n_n
    first, pace = 4, max(1, (spots - 4) // (len(events) + 1))
    at_spot = {}
    for e, event in enumerate(events):
        place = first + e * pace
        at_spot.setdefault(place if place < spots else None, []).append(event)

    def block(m, carry):
        left_t[...] = left[:, pl.ds(pl.multiple_of(m * ROWS, ROWS), ROWS)].T
        arow = m // per_arow
        c_at = pl.multiple_of((m % per_arow) * ROWS, ROWS)
        for n in range(n_n):
            value = jnp.dot(
                left_t[...], right[:, n * COLS:(n + 1) * COLS], preferred_element_type=jnp.float32
            )
            top = value.astype(jnp.bfloat16)
            rest = (value - top.astype(jnp.float32)).astype(jnp.bfloat16)
            for b in range(COLS // dsl):
                at = arow * window + n * (COLS // dsl) + b
                high[at, pl.ds(c_at, ROWS), :] = top[:, b * dsl:(b + 1) * dsl]
                low[at, pl.ds(c_at, ROWS), :] = rest[:, b * dsl:(b + 1) * dsl]
            for place, todo in at_spot.items():
                if place is not None and place % n_n == n:
                    @pl.when(m == place // n_n)
                    def _(todo=todo):
                        for event in todo:
                            event()
        return carry

    lax.fori_loop(0, n_m, block, 0)
    for event in at_spot.get(None, []):
        event()
    keep.wait()
    for k in every:
        for j in range(n_hi):
            for i in range(n_aux):
                arrive(("c", k, j, i), k, j, i, True)

    span = GROUP * 4
    rows = min(pairs, 16)
    for p in range(0, pairs, rows):
        acc[...] = jnp.zeros_like(acc)

        def contract(g, carry):
            def gathered(ref, lead, count):
                return jnp.concatenate(
                    [
                        ref[pl.ds(lead, count), pl.ds(pl.multiple_of(g * span + q * GROUP, GROUP), GROUP), :]
                        .reshape(count * GROUP, dsl)
                        for q in range(span // GROUP)
                    ],
                    axis=1,
                )

            amp = gathered(tbuf, p, rows)
            dims = (((1,), (1,)), ((), ()))
            acc[...] += lax.dot_general(
                amp, gathered(high, 0, rows_ab), dims, preferred_element_type=jnp.float32
            ) + lax.dot_general(
                amp, gathered(low, 0, rows_ab), dims, preferred_element_type=jnp.float32
            )
            return carry

        lax.fori_loop(0, virt // span, contract, 0)
        shape = acc.shape
        row = lax.broadcasted_iota(jnp.int32, shape, 0) % GROUP
        col = lax.broadcasted_iota(jnp.int32, shape, 1) % GROUP
        diag = jnp.where(row == col, acc[...], 0.0)
        diag = jnp.sum(diag.reshape(rows, GROUP, shape[1]), axis=1)
        pick = (
            lax.broadcasted_iota(jnp.int32, (shape[1], LANES), 0) // GROUP
            == lax.broadcasted_iota(jnp.int32, (shape[1], LANES), 1)
        ).astype(jnp.float32)
        parts[0, pl.ds(p, rows), :] = jnp.dot(
            diag, pick, precision=lax.Precision.HIGHEST, preferred_element_type=jnp.float32
        )

    per = other_ref.shape[0]
    mine = occ * n_aux + aux
    base = mine * per
    row = lax.broadcasted_iota(jnp.int32, (pairs, LANES), 0)
    whole = parts[0]
    for r in range(per):
        whole = whole + jnp.where(row == base + r, other_ref[r:r + 1, :], 0.0)
    members = n_occ * n_aux
    parts[1 + mine] = whole
    started = []
    for number, (k, i) in enumerate(group):
        copy = pltpu.make_async_remote_copy(
            src_ref=parts.at[1 + mine], dst_ref=parts.at[1 + mine],
            send_sem=part_send.at[number], recv_sem=part_recv.at[number],
            device_id={"occ": turn(occ, k, n_occ), "aux": turn(aux, i, n_aux)}, device_id_type=MESH,
        )
        copy.start()
        started.append(copy)
    assert len(sent) == len(numbers) - 1
    for copy in sent:
        copy.wait_send()
    for number, (k, i) in enumerate(group):
        ref = parts.at[1 + turn(occ, -k, n_occ) * n_aux + turn(aux, -i, n_aux)]
        pltpu.make_async_remote_copy(
            src_ref=ref, dst_ref=ref, send_sem=part_send.at[number], recv_sem=part_recv.at[number],
            device_id={"occ": turn(occ, k, n_occ), "aux": turn(aux, i, n_aux)}, device_id_type=MESH,
        ).wait_recv()
    total = parts[1]
    for g in range(1, members):
        total = total + parts[1 + g]
    squares = jnp.sum(jnp.sum(total * total, axis=0, keepdims=True), axis=1, keepdims=True)
    norms[sec] = jnp.broadcast_to(squares, (1, LANES))
    for j in range(1, n_sec):
        copy = pltpu.make_async_remote_copy(
            src_ref=norms.at[sec], dst_ref=norms.at[sec],
            send_sem=norm_send.at[j], recv_sem=norm_recv.at[j],
            device_id={"vsec": turn(sec, j, n_sec)}, device_id_type=MESH,
        )
        copy.start()
        started.append(copy)
    for r in range(per):
        res_ref[r:r + 1, :] = jnp.sum(
            jnp.where(row == base + r, total, 0.0), axis=0, keepdims=True
        )
    for j in range(1, n_sec):
        ref = norms.at[turn(sec, -j, n_sec)]
        pltpu.make_async_remote_copy(
            src_ref=ref, dst_ref=ref, send_sem=norm_send.at[j], recv_sem=norm_recv.at[j],
            device_id={"vsec": turn(sec, j, n_sec)}, device_id_type=MESH,
        ).wait_recv()
    squares = norms[0]
    for j in range(1, n_sec):
        squares = squares + norms[j]
    norm_ref[...] = jnp.sqrt(squares)
    for copy in started:
        copy.wait_send()


def on_device(sizes, amplitudes, left_factor, right_factor, other_terms):
    n_occ, n_sec, n_aux = sizes
    aux_rows, arow_count, virt = left_factor.shape
    window, dsl = right_factor.shape[1:]
    pairs = n_occ * n_sec
    per = other_terms.shape[0]
    ab = arow_count * window
    left = left_factor.reshape(aux_rows, arow_count * virt)
    right = right_factor.reshape(aux_rows, window * dsl)
    other = jnp.pad(other_terms.reshape(per, ab), ((0, 0), (0, LANES - ab)))
    copies = pairs * n_aux
    members = n_occ * n_aux
    rows = min(pairs, 16)
    dma = pltpu.SemaphoreType.DMA
    vmem = pl.BlockSpec(memory_space=pltpu.VMEM)
    anywhere = pl.BlockSpec(memory_space=pl.ANY)
    res, norm = pl.pallas_call(
        functools.partial(ladder_kernel, sizes),
        out_shape=(
            jax.ShapeDtypeStruct((per, LANES), jnp.float32),
            jax.ShapeDtypeStruct((1, LANES), jnp.float32),
        ),
        in_specs=[vmem, anywhere, anywhere, vmem],
        out_specs=(vmem, vmem),
        scratch_shapes=[
            pltpu.VMEM((pairs, virt, dsl), jnp.bfloat16),
            pltpu.VMEM(left.shape, jnp.bfloat16),
            pltpu.VMEM(right.shape, jnp.bfloat16),
            pltpu.VMEM((ROWS, aux_rows), jnp.bfloat16),
            pltpu.VMEM((ab, virt, dsl), jnp.bfloat16),
            pltpu.VMEM((ab, virt, dsl), jnp.bfloat16),
            pltpu.VMEM((rows * GROUP, ab * GROUP), jnp.float32),
            pltpu.VMEM((1 + members, pairs, LANES), jnp.float32),
            pltpu.VMEM((n_sec, 1, LANES), jnp.float32),
            dma((copies,)), dma((copies,)), dma((3,)),
            dma((members,)), dma((members,)), dma((n_sec,)), dma((n_sec,)),
        ],
        compiler_params=pltpu.CompilerParams(
            collective_id=0, has_side_effects=True, vmem_limit_bytes=64000 * 1024
        ),
    )(amplitudes, left, right, other)
    return res[:, :ab].reshape(other_terms.shape), norm[0, 0]


def solution(mesh):
    placed = (
        P(("occ", "vsec"), "aux", None),
        P("aux", "vsec", None),
        P("aux", None, "occ"),
        P(("occ", "aux"), "vsec", None),
    )
    sizes = (mesh.shape["occ"], mesh.shape["vsec"], mesh.shape["aux"])
    return jax.shard_map(
        functools.partial(on_device, sizes),
        mesh=mesh,
        in_specs=placed,
        out_specs=(P(("occ", "aux"), "vsec", None), P()),
        check_vma=False,
    )
```

profile of v0, /device:TPU:0, one launch (start us, length us, event | category | flops | bytes accessed | tf_op | source)
XLA Modules:
  0.0 96.6 jit_solution(13244042929044600232)
XLA Ops:
  0.6 0.8 reshape.18
  1.4 0.6 pad.4.other_ref
  2.0 10.1 %copy.6 = bf16[256,8,2,1024]{3,1,2,0:T(8,128)(2,1)} copy(bf16[256,8,2,1024]{3,2,1,0:T(2,128)(2,1)} %bitcast.9) | data formatting | bytes 16777216
  12.1 10.3 %copy.7 = bf16[256,8,8,256]{3,1,2,0:T(8,128)(2,1)} copy(bf16[256,8,8,256]{3,2,1,0:T(8,128)(2,1)} %bitcast.10) | data formatting | bytes 16777216
  22.4 71.1 %shard_map.59 = (f32[2,128]{1,0:T(2,128)}, f32[1,128]{1,0:T(1,128)}) custom-call(bf16[1,512,1024]{2,1,0:T(8,128)(2,1)} %amps_ref.1, bf16[2048,2048]{1,0:T(8,128)(2,1)} %bitcast.7, bf16[2048,2048]{1,0:T(8,128)(2,1)} %bitcast.8, f32[2,128]{1,0:T(2,128)} %pad.4.other_ref), custom_call_target="tpu_custom_call" | custom-call | tf_op jit(solution)/shard_map/pallas_call | solution.py:312
  93.5 1.3 %reshape.19 = f32[2,2,8]{2,1,0:T(2,128)} reshape(f32[2,16]{1,0:T(2,128)} %bitcast.11) | data formatting | bytes 256 | tf_op jit(solution)/shard_map/reshape | solution.py:337
where the time goes:
time: 96.8 us; the launch traced here: 96.6 us
  Pallas kernels  71.1 us (73%)
  local copies, waits for them, and re-layouts  23.1 us (24%)
  between operations  2.38 us (2%)
    pallas_call x1, Pallas kernels, on_device(): pl.pallas_call(functools.partial(ladder_kernel, sizes), out_shape=(jax.Sh...  71.1 us
    unnamed x2, local copies, waits for them, and re-layouts  20.4 us

commit v1 on v0

--- a/solution.py
+++ b/solution.py
@@ -16,7 +16,7 @@
 
 def ladder_kernel(
     sizes, amps_ref, left_hbm, right_hbm, other_ref, res_ref, norm_ref,
-    tbuf, left, right, left_t, high, low, acc, parts, norms,
+    tbuf, left, right_in, right, left_t, high, low, acc, parts, norms,
     send_sem, recv_sem, load_sem, part_send, part_recv, norm_send, norm_recv,
 ):
     n_occ, n_sec, n_aux = sizes
@@ -30,7 +30,7 @@
     rows_ab = high.shape[0]
 
     load_l = pltpu.make_async_copy(left_hbm, left, load_sem.at[0])
-    load_r = pltpu.make_async_copy(right_hbm, right, load_sem.at[1])
+    load_r = pltpu.make_async_copy(right_hbm, right_in, load_sem.at[1])
     load_l.start()
     load_r.start()
 
@@ -156,27 +156,41 @@
 
     load_l.wait()
     load_r.wait()
-    n_m, n_n = left.shape[1] // ROWS, wide // COLS
-    per_arow = virt // ROWS
+    early = 3
+    for event in events[:early]:
+        event()
+    events = events[early:]
+    aux_rows, arow_count = left.shape[:2]
+    n_m, n_col = virt // ROWS, wide // COLS
+    n_n = arow_count * n_col
     spots = n_m * n_n
-    first, pace = 4, max(1, (spots - 4) // (len(events) + 1))
+
+    def flatten(step, carry):
+        at = pl.ds(pl.multiple_of(step * ROWS, ROWS), ROWS)
+        for b in range(window):
+            right[at, b * dsl:(b + 1) * dsl] = right_in[at, b, :]
+        return carry
+
+    lax.fori_loop(0, aux_rows // ROWS, flatten, 0)
+    first, pace = 0, max(1, spots // max(1, len(events)))
     at_spot = {}
     for e, event in enumerate(events):
         place = first + e * pace
         at_spot.setdefault(place if place < spots else None, []).append(event)
 
     def block(m, carry):
-        left_t[...] = left[:, pl.ds(pl.multiple_of(m * ROWS, ROWS), ROWS)].T
-        arow = m // per_arow
-        c_at = pl.multiple_of((m % per_arow) * ROWS, ROWS)
+        c_at = pl.multiple_of(m * ROWS, ROWS)
         for n in range(n_n):
+            arow, col = n // n_col, n % n_col
+            if col == 0:
+                left_t[...] = left[:, arow, pl.ds(c_at, ROWS)].T
             value = jnp.dot(
-                left_t[...], right[:, n * COLS:(n + 1) * COLS], preferred_element_type=jnp.float32
+                left_t[...], right[:, col * COLS:(col + 1) * COLS], preferred_element_type=jnp.float32
             )
             top = value.astype(jnp.bfloat16)
             rest = (value - top.astype(jnp.float32)).astype(jnp.bfloat16)
             for b in range(COLS // dsl):
-                at = arow * window + n * (COLS // dsl) + b
+                at = arow * window + col * (COLS // dsl) + b
                 high[at, pl.ds(c_at, ROWS), :] = top[:, b * dsl:(b + 1) * dsl]
                 low[at, pl.ds(c_at, ROWS), :] = rest[:, b * dsl:(b + 1) * dsl]
             for place, todo in at_spot.items():
@@ -300,8 +314,6 @@
     pairs = n_occ * n_sec
     per = other_terms.shape[0]
     ab = arow_count * window
-    left = left_factor.reshape(aux_rows, arow_count * virt)
-    right = right_factor.reshape(aux_rows, window * dsl)
     other = jnp.pad(other_terms.reshape(per, ab), ((0, 0), (0, LANES - ab)))
     copies = pairs * n_aux
     members = n_occ * n_aux
@@ -319,8 +331,9 @@
         out_specs=(vmem, vmem),
         scratch_shapes=[
             pltpu.VMEM((pairs, virt, dsl), jnp.bfloat16),
-            pltpu.VMEM(left.shape, jnp.bfloat16),
-            pltpu.VMEM(right.shape, jnp.bfloat16),
+            pltpu.VMEM(left_factor.shape, jnp.bfloat16),
+            pltpu.VMEM(right_factor.shape, jnp.bfloat16),
+            pltpu.VMEM((aux_rows, window * dsl), jnp.bfloat16),
             pltpu.VMEM((ROWS, aux_rows), jnp.bfloat16),
             pltpu.VMEM((ab, virt, dsl), jnp.bfloat16),
             pltpu.VMEM((ab, virt, dsl), jnp.bfloat16),
@@ -333,7 +346,7 @@
         compiler_params=pltpu.CompilerParams(
             collective_id=0, has_side_effects=True, vmem_limit_bytes=64000 * 1024
         ),
-    )(amplitudes, left, right, other)
+    )(amplitudes, left_factor, right_factor, other)
     return res[:, :ab].reshape(other_terms.shape), norm[0, 0]
 
 

time: 96.8 us -> 95.3 us (0.985)
  local copies, waits for them, and re-layouts: 23.1 us -> 2.65 us
  Pallas kernels: 71.1 us -> 90 us
    unnamed x2 -> x0, local copies, waits for them, and re-layouts: 20.4 us -> none
    pallas_call x1, Pallas kernels: 71.1 us -> 90 us  [on_device(): pl.pallas_call(functools.partial(ladder_kernel, sizes), out_shape=(jax.Sh...]
where the time goes in v1:
time: 95.3 us; the launch traced here: 95.1 us
  Pallas kernels  90 us (94%)
  local copies, waits for them, and re-layouts  2.65 us (3%)
  between operations  2.4 us (3%)
    pallas_call x1, Pallas kernels, on_device(): pl.pallas_call(functools.partial(ladder_kernel, sizes), out_shape=(jax.Sh...  90 us

profile of v1, /device:TPU:0, one launch (start us, length us, event | category | flops | bytes accessed | tf_op | source)
XLA Modules:
  0.0 95.1 jit_solution(14307971347221014775)
XLA Ops:
  0.6 0.8 reshape.10
  1.4 0.6 pad.4.other_ref
  2.0 90.0 %shard_map.59 = (f32[2,128]{1,0:T(2,128)}, f32[1,128]{1,0:T(1,128)}) custom-call(bf16[1,512,1024]{2,1,0:T(8,128)(2,1)} %amps_ref.1, bf16[2048,2,1024]{2,1,0:T(2,128)(2,1)} %left_hbm.1, bf16[2048,8,256]{2,1,0:T(8,128)(2,1)} %right_hbm.1, f32[2,128]{1,0:T(2,128)} %pad.4.other_ref), custom_call_target="tpu_custom_call" | custom-call | tf_op jit(solution)/shard_map/pallas_call | solution.py:324
  92.0 1.3 %reshape.11 = f32[2,2,8]{2,1,0:T(2,128)} reshape(f32[2,16]{1,0:T(2,128)} %bitcast.3) | data formatting | bytes 256 | tf_op jit(solution)/shard_map/reshape | solution.py:350
